TPU v7x, 32 devices: a whole 2x2x4 slice. The times are simulated.
32 devices in a mesh: grp: 2 (over x), ha: 16 (over z, y, core).
Axes of the slice: x: 2, y: 2, z: 4, core: 2. Of those that a mesh axis runs over, the one named last changes fastest.
Arguments:
- frames: bfloat16 [4, 16, 112, 384], P('grp', 'ha'), parts along dimension 0, may hold values from -6 to 6
- cache_first: bfloat16 [4, 16, 112, 384], P('grp', 'ha'), parts along dimension 0, may hold values from -5 to 5
- cache_second: bfloat16 [4, 16, 112, 384], P('grp', 'ha'), parts along dimension 0, may hold values from -5 to 5
- gain_first: float32 [384], replicated, may hold values from 0.1 to 1.9
- gain_second: float32 [384], replicated, may hold values from 0.1 to 1.9
- bias_first: float32 [384], replicated, may hold values from -3 to 3
- bias_second: float32 [384], replicated, may hold values from -3 to 3
- weight_first: bfloat16 [10368, 384], P(None, 'ha'), may hold values from -0.0625 to 0.0625
- weight_second: bfloat16 [10368, 384], P(None, 'ha'), may hold values from -0.0625 to 0.0625
- cotangent: bfloat16 [4, 16, 112, 384], P('grp', 'ha'), parts along dimension 0, may hold values from -6 to 6
Outputs:
- output: bfloat16 [4, 16, 112, 384], P('grp', 'ha'), parts along dimension 0
- grad_frames: bfloat16 [4, 16, 112, 384], P('grp', 'ha'), parts along dimension 0
There are 2 independent parts, one for each index of `grp`. A program takes and returns all parts, laid end to end along the dimension named above; an argument that names none is the same for every part. Nothing has to cross between parts.
All inputs are finite; a program needn't handle non-finite values.
Results may differ from a plain program's by a relative error of at most 0.006.
Values may be sent and summed in bfloat16 or wider, within the bound.
No kernel may reach another device: no remote copies, remote signals or barrier semaphores. Data moves between devices by JAX's collectives and lax.ppermute only.
A program may use at most 128 MiB of HBM per device.

v0:
```python
import jax
import jax.numpy as jnp
from jax import lax
from jax.sharding import PartitionSpec as P


def extended_2(block, sides, width):
    for axis, dim in sides:
        count = lax.axis_size(axis)
        forward = [(i, i + 1) for i in range(count - 1)]
        backward = [(target, source) for source, target in forward]
        low = lax.ppermute(
            lax.slice_in_dim(block, block.shape[dim] - width, None, axis=dim), axis, forward
        )
        high = lax.ppermute(lax.slice_in_dim(block, 0, width, axis=dim), axis, backward)
        block = jnp.concatenate([low, block, high], axis=dim)
    return block


def normed_silu(values, scales):
    mean_square = jnp.mean(values * values, axis=-1, keepdims=True)
    inverse = lax.rsqrt(mean_square + 1e-06)
    normed = values * inverse * scales
    return normed * jax.nn.sigmoid(normed)


def silu_backward(values, scales, upstream):
    mean_square = jnp.mean(values * values, axis=-1, keepdims=True)
    inverse = lax.rsqrt(mean_square + 1e-06)
    normed = values * inverse * scales
    sigmoid_value = jax.nn.sigmoid(normed)
    scaled = scales * upstream * sigmoid_value * (1.0 + normed * (1.0 - sigmoid_value))
    return inverse * scaled - values * inverse**3 * jnp.mean(
        values * scaled, axis=-1, keepdims=True
    )


def tap_patches(padded, length, rows, columns, flipped):
    pieces = []
    for frame_tap in range(3):
        for row_tap in range(3):
            for col_tap in range(3):
                if flipped:
                    frame_start, row_start, col_start = (2 - frame_tap, 2 - row_tap, 2 - col_tap)
                else:
                    frame_start, row_start, col_start = (frame_tap, row_tap, col_tap)
                pieces.append(
                    padded[
                        frame_start : frame_start + length,
                        row_start : row_start + rows,
                        col_start : col_start + columns,
                    ]
                )
    return jnp.stack(pieces, axis=3)


def local(
    frames,
    cache_first,
    cache_second,
    gain_first,
    gain_second,
    bias_first,
    bias_second,
    weight_first,
    weight_second,
    cotangent,
):
    length, rows, columns, channels = frames.shape
    kernel_one, kernel_two = (
        lax.all_gather(weight_first, "ha", axis=1, tiled=True),
        lax.all_gather(weight_second, "ha", axis=1, tiled=True),
    )
    kernel_one = kernel_one.reshape(27, channels, channels)
    inputs = frames.astype(jnp.float32)
    first_act = normed_silu(inputs, gain_first).astype(jnp.bfloat16)
    extended = jnp.concatenate([cache_first, first_act], axis=0)
    padded = extended_2(extended, (("ha", 1),), 1)
    padded = jnp.pad(padded, ((0, 0), (0, 0), (1, 1), (0, 0)))
    patches = tap_patches(padded, length, rows, columns, False)
    middle = jnp.einsum("lrwtc,tco->lrwo", patches, kernel_one, preferred_element_type=jnp.float32)
    middle = (middle + bias_first).astype(jnp.bfloat16)
    middle_float = middle.astype(jnp.float32)
    kernel_two = kernel_two.reshape(27, channels, channels)
    second_act = normed_silu(middle_float, gain_second).astype(jnp.bfloat16)
    extended = jnp.concatenate([cache_second, second_act], axis=0)
    padded = extended_2(extended, (("ha", 1),), 1)
    padded = jnp.pad(padded, ((0, 0), (0, 0), (1, 1), (0, 0)))
    patches = tap_patches(padded, length, rows, columns, False)
    second_out = jnp.einsum(
        "lrwtc,tco->lrwo", patches, kernel_two, preferred_element_type=jnp.float32
    )
    output = (inputs + second_out + bias_second).astype(jnp.bfloat16)
    padded = extended_2(cotangent, (("ha", 1),), 1)
    padded = jnp.pad(padded, ((0, 2), (0, 0), (1, 1), (0, 0)))
    patches = tap_patches(padded, length, rows, columns, True)
    grad_second = jnp.einsum(
        "lrwto,tco->lrwc", patches, kernel_two, preferred_element_type=jnp.float32
    )
    grad_middle = silu_backward(middle_float, gain_second, grad_second).astype(jnp.bfloat16)
    padded = extended_2(grad_middle, (("ha", 1),), 1)
    padded = jnp.pad(padded, ((0, 2), (0, 0), (1, 1), (0, 0)))
    patches = tap_patches(padded, length, rows, columns, True)
    grad_first = jnp.einsum(
        "lrwto,tco->lrwc", patches, kernel_one, preferred_element_type=jnp.float32
    )
    grad_frames = (
        cotangent.astype(jnp.float32) + silu_backward(inputs, gain_first, grad_first)
    ).astype(jnp.bfloat16)
    return (output, grad_frames)


def solution(mesh):
    return jax.shard_map(
        local,
        mesh=mesh,
        in_specs=(
            P("grp", "ha", None, None),
            P("grp", "ha", None, None),
            P("grp", "ha", None, None),
            P(),
            P(),
            P(),
            P(),
            P(None, "ha"),
            P(None, "ha"),
            P("grp", "ha", None, None),
        ),
        out_specs=(P("grp", "ha", None, None), P("grp", "ha", None, None)),
        check_vma=False,
    )
```

profile of v0, /device:TPU:5, one launch (start us, length us, event | category | flops | bytes accessed | tf_op | source)
XLA Modules:
  0.0 222.6 jit_solution(1379792984267743407)
XLA Ops:
  8.7 1.0 fusion.91
  9.7 1.1 fusion.99
  10.8 1.0 pad_maximum_fusion
  11.8 2.6 %collective-permute-start.1 = (bf16[4,1,112,384]{3,2,0,1:T(8,128)(2,1)S(1)}, bf16[4,1,112,384]{3,2,0,1:T(8,128)(2,1)S(1)}, u32[]{:S(2)}, u32[]{:S(2)}) collective-permute-start(bf16[4,1,112,384]{3,2,0,1:T(8,128)(2,1)S(1)} %pad_maximum_fusion), channel_id=1, source_target_pairs={{1,0},{2,1},{3,2},{4,3},{5,4},{6,5},{7,6},{8,7},{9,8},{10,9},{11,1... | collective-permute-start | bytes 1032200 | tf_op jit(solution)/shard_map/ppermute | solution.py:15
  14.4 3.9 %collective-permute-start = (bf16[4,1,112,384]{3,2,0,1:T(8,128)(2,1)S(1)}, bf16[4,1,112,384]{3,2,0,1:T(8,128)(2,1)S(1)}, u32[]{:S(2)}, u32[]{:S(2)}) collective-permute-start(bf16[4,1,112,384]{3,2,0,1:T(8,128)(2,1)S(1)} %pad_maximum_fusion), channel_id=1, source_target_pairs={{0,1},{1,2},{2,3},{3,4},{4,5},{5,6},{6,7},{7,8},{8,9},{9,10},{10,1... | collective-permute-start | bytes 1032200 | tf_op jit(solution)/shard_map/ppermute | solution.py:12
  18.3 1.9 collective-permute-start.5
  20.2 4.5 %collective-permute-start.4 = (bf16[2,1,112,384]{3,2,0,1:T(8,128)(2,1)}, bf16[2,1,112,384]{3,2,0,1:T(8,128)(2,1)S(1)}, u32[]{:S(2)}, u32[]{:S(2)}) collective-permute-start(bf16[2,1,112,384]{3,2,0,1:T(8,128)(2,1)} %bitcast.545), channel_id=1, source_target_pairs={{0,1},{1,2},{2,3},{3,4},{4,5},{5,6},{6,7},{7,8},{8,9},{9,10},{10,1... | collective-permute-start | bytes 516104 | tf_op jit(solution)/shard_map/ppermute | solution.py:12
  30.5 0.8 collective-permute-done.5
  32.9 1.1 constant_dynamic-update-slice_fusion.26
  33.9 0.8 constant_dynamic-update-slice_fusion.25
  34.7 0.7 constant_dynamic-update-slice_fusion.24
  35.4 0.7 constant_dynamic-update-slice_fusion.23
  36.1 0.7 constant_dynamic-update-slice_fusion.22
  36.8 0.7 constant_dynamic-update-slice_fusion.21
  37.6 0.7 constant_dynamic-update-slice_fusion.20
  38.3 0.7 constant_dynamic-update-slice_fusion.19
  39.0 0.7 constant_dynamic-update-slice_fusion.18
  40.4 0.7 constant_dynamic-update-slice_fusion.16
  41.1 0.7 constant_dynamic-update-slice_fusion.15
  42.5 0.7 constant_dynamic-update-slice_fusion.13
  43.2 0.7 constant_dynamic-update-slice_fusion.12
  45.3 0.7 constant_dynamic-update-slice_fusion.9
  47.4 0.7 constant_dynamic-update-slice_fusion.6
  48.8 0.9 constant_dynamic-update-slice_fusion.4
  49.6 0.7 constant_dynamic-update-slice_fusion.3
  51.7 0.7 constant_dynamic-update-slice_fusion
  52.5 33.8 %all-gather.3.cloned.1.call-done = bf16[10368,384]{0,1:T(8,128)(2,1)} async-done(((bf16[10368,24]{0,1:T(8,128)(2,1)}), bf16[10368,384]{0,1:T(8,128)(2,1)}) %all-gather.3.cloned.1.call-update) | async-done | bytes 7962640 | tf_op jit(solution)/shard_map/all_gather | solution.py:71
  86.2 11.3 %copy.39 = bf16[10368,384]{1,0:T(8,128)(2,1)} copy(bf16[10368,384]{0,1:T(8,128)(2,1)} %all-gather.3.cloned.1.call-done) | data formatting | bytes 15925248 | tf_op jit(solution)/shard_map/all_gather | solution.py:71
  97.6 7.4 %multiply_reduce_fusion.1 = (f32[2,112]{1,0:T(2,128)S(1)}, f32[2,112,384]{2,1,0:T(8,128)S(1)}) fusion(f32[384]{0:T(512)S(1)} %copy-done.7, bf16[27,384,384,1]{2,1,0,3:T(8,128)(2,1)} %bitcast.528, bf16[2,1,112,27,384]{4,2,3,0,1:T(8,128)(2,1)} %constant_dynamic-update-slice_fusion), kind=kOutput, calls=%fused_computation.90 | convolution fusion | flops 1784057600 | bytes 12953984 | tf_op jit(solution)/shard_map/lrwtc,tco->lrwo/dot_general | solution.py:81
  105.0 53.7 %all-gather.5.cloned.1.call-done = bf16[10368,384]{0,1:T(8,128)(2,1)} async-done(((bf16[10368,24]{0,1:T(8,128)(2,1)}), bf16[10368,384]{0,1:T(8,128)(2,1)}) %all-gather.5.cloned.1.call-update) | async-done | bytes 7962640 | tf_op jit(solution)/shard_map/all_gather | solution.py:72
  158.7 11.3 %copy.41 = bf16[10368,384]{1,0:T(8,128)(2,1)} copy(bf16[10368,384]{0,1:T(8,128)(2,1)} %all-gather.5.cloned.1.call-done) | data formatting | bytes 15925248 | tf_op jit(solution)/shard_map/all_gather | solution.py:72
  170.0 7.7 %multiply_reduce_fusion = (f32[2,112]{1,0:T(2,128)S(1)}, f32[2,112,384]{2,1,0:T(8,128)S(1)}) fusion(f32[2,112,384]{2,1,0:T(8,128)S(1)} %get-tuple-element.11, f32[2,112]{1,0:T(2,128)S(1)} %get-tuple-element.9, bf16[27,384,384,1]{2,1,3,0:T(8,128)(2,1)} %bitcast.524, bf16[2,1,112,27,384]{4,2,0,3,1:T(8,128)(2,1)} %copy-done.5, f32[384]{0:T(512)S(1)} %copy-done.6), kind=kOutput, calls=%fused_computation.86 | convolution fusion | flops 1784745728 | bytes 13298944 | tf_op jit(solution)/shard_map/lrwto,tco->lrwc/dot_general | solution.py:97
  178.0 2.2 collective-permute-start.7
  180.2 4.3 %collective-permute-start.6 = (bf16[2,1,112,384]{3,2,0,1:T(8,128)(2,1)S(1)}, bf16[2,1,112,384]{3,2,0,1:T(8,128)(2,1)S(1)}, u32[]{:S(2)}, u32[]{:S(2)}) collective-permute-start(bf16[2,1,112,384]{3,2,0,1:T(8,128)(2,1)S(1)} %bitcast.542), channel_id=1, source_target_pairs={{0,1},{1,2},{2,3},{3,4},{4,5},{5,6},{6,7},{7,8},{8,9},{9,10},{10,1... | collective-permute-start | bytes 516104 | tf_op jit(solution)/shard_map/ppermute | solution.py:12
  185.2 1.9 collective-permute-start.3
  187.1 4.7 %collective-permute-start.2 = (bf16[4,1,112,384]{3,2,0,1:T(8,128)(2,1)S(1)}, bf16[4,1,112,384]{3,2,0,1:T(8,128)(2,1)S(1)}, u32[]{:S(2)}, u32[]{:S(2)}) collective-permute-start(bf16[4,1,112,384]{3,2,0,1:T(8,128)(2,1)S(1)} %pad_maximum_fusion.1), channel_id=1, source_target_pairs={{0,1},{1,2},{2,3},{3,4},{4,5},{5,6},{6,7},{7,8},{8,9},{9,10},{10,1... | collective-permute-start | bytes 1032200 | tf_op jit(solution)/shard_map/ppermute | solution.py:12
  192.0 0.7 constant_dynamic-update-slice_fusion.98
  192.8 0.7 constant_dynamic-update-slice_fusion.97
  194.1 0.7 constant_dynamic-update-slice_fusion.95
  194.9 0.7 constant_dynamic-update-slice_fusion.94
  196.3 0.7 constant_dynamic-update-slice_fusion.92
  197.0 0.7 constant_dynamic-update-slice_fusion.91
  198.4 0.7 constant_dynamic-update-slice_fusion.89
  200.5 0.7 constant_dynamic-update-slice_fusion.86
  202.5 0.7 constant_dynamic-update-slice_fusion.83
  204.7 5.4 %fusion.105 = (f32[2,112]{1,0:T(2,128)S(1)}, f32[2,1,112,384]{3,2,0,1:T(8,128)S(1)}) fusion(bf16[2,1,112,384]{3,2,1,0:T(8,128)(2,1)S(1)} %copy-done, f32[384]{0:T(512)S(1)} %copy-done.4, f32[2,112]{1,0:T(2,128)S(1)} %get-tuple-element.7, bf16[27,384,384,1]{2,1,3,0:T(8,128)(2,1)S(1)} %bitcast.531, ...), kind=kOutput, calls=%fused_computation.84 | convolution fusion | flops 1784831744 | bytes 13126912 | tf_op jit(solution)/shard_map/lrwto,tco->lrwc/dot_general | solution.py:104
  210.0 0.8 fusion.106
  212.5 3.3 %fusion.68 = bf16[2,1,112,384]{3,2,1,0:T(8,128)(2,1)} fusion(bf16[27,384,384,1]{2,1,3,0:T(8,128)(2,1)S(1)} %bitcast.527, bf16[2,1,112,27,384]{4,2,0,3,1:T(8,128)(2,1)S(1)} %constant_dynamic-update-slice_fusion.27, bf16[2,1,112,384]{3,2,1,0:T(8,128)(2,1)S(1)} %copy-done, f32[384]{0:T(512)S(1)} %copy-done.8), kind=kOutput, calls=%fused_computation.37 | convolution fusion | flops 1783971840 | bytes 12953088 | tf_op jit(solution)/shard_map/lrwtc,tco->lrwo/dot_general | solution.py:90
  (130 shorter events, 23.4 us)
Async XLA Ops:
  7.2 24.3 %copy-start.3 = (bf16[2,1,112,384]{3,2,1,0:T(8,128)(2,1)S(1)}, bf16[2,1,112,384]{3,2,1,0:T(8,128)(2,1)}, u32[]{:S(2)}) copy-start(bf16[2,1,112,384]{3,2,1,0:T(8,128)(2,1)} %param.19) | copy-start | bytes 516100
  7.2 79.1 %all-gather.3.cloned.1.call-start = ((), (), s32[]{:S(2)}) async-start(), calls=%async_computation | async-start | bytes 8460288 | tf_op jit(solution)/shard_map/all_gather | solution.py:71
  7.9 150.8 %all-gather.5.cloned.1.call-start = ((), (), s32[]{:S(2)}) async-start(), calls=%async_computation.1 | async-start | bytes 8460288 | tf_op jit(solution)/shard_map/all_gather | solution.py:72
  11.8 20.7 %collective-permute-start.1 = (bf16[4,1,112,384]{3,2,0,1:T(8,128)(2,1)S(1)}, bf16[4,1,112,384]{3,2,0,1:T(8,128)(2,1)S(1)}, u32[]{:S(2)}, u32[]{:S(2)}) collective-permute-start(bf16[4,1,112,384]{3,2,0,1:T(8,128)(2,1)S(1)} %pad_maximum_fusion), channel_id=1, source_target_pairs={{1,0},{2,1},{3,2},{4,3},{5,4},{6,5},{7,6},{8,7},{9,8},{10,9},{11,1... | collective-permute-start | bytes 1032200 | tf_op jit(solution)/shard_map/ppermute | solution.py:15
  14.4 18.2 %collective-permute-start = (bf16[4,1,112,384]{3,2,0,1:T(8,128)(2,1)S(1)}, bf16[4,1,112,384]{3,2,0,1:T(8,128)(2,1)S(1)}, u32[]{:S(2)}, u32[]{:S(2)}) collective-permute-start(bf16[4,1,112,384]{3,2,0,1:T(8,128)(2,1)S(1)} %pad_maximum_fusion), channel_id=1, source_target_pairs={{0,1},{1,2},{2,3},{3,4},{4,5},{5,6},{6,7},{7,8},{8,9},{9,10},{10,1... | collective-permute-start | bytes 1032200 | tf_op jit(solution)/shard_map/ppermute | solution.py:12
  18.3 13.0 %collective-permute-start.5 = (bf16[2,1,112,384]{3,2,0,1:T(8,128)(2,1)}, bf16[2,1,112,384]{3,2,0,1:T(8,128)(2,1)S(1)}, u32[]{:S(2)}, u32[]{:S(2)}) collective-permute-start(bf16[2,1,112,384]{3,2,0,1:T(8,128)(2,1)} %bitcast.544), channel_id=1, source_target_pairs={{1,0},{2,1},{3,2},{4,3},{5,4},{6,5},{7,6},{8,7},{9,8},{10,9},{11,1... | collective-permute-start | bytes 516104 | tf_op jit(solution)/shard_map/ppermute | solution.py:15
  20.2 11.2 %collective-permute-start.4 = (bf16[2,1,112,384]{3,2,0,1:T(8,128)(2,1)}, bf16[2,1,112,384]{3,2,0,1:T(8,128)(2,1)S(1)}, u32[]{:S(2)}, u32[]{:S(2)}) collective-permute-start(bf16[2,1,112,384]{3,2,0,1:T(8,128)(2,1)} %bitcast.545), channel_id=1, source_target_pairs={{0,1},{1,2},{2,3},{3,4},{4,5},{5,6},{6,7},{7,8},{8,9},{9,10},{10,1... | collective-permute-start | bytes 516104 | tf_op jit(solution)/shard_map/ppermute | solution.py:12
  25.6 6.9 %copy-start.1 = (bf16[2,1,112,384]{3,2,1,0:T(8,128)(2,1)S(1)}, bf16[2,1,112,384]{3,2,1,0:T(8,128)(2,1)}, u32[]{:S(2)}) copy-start(bf16[2,1,112,384]{3,2,1,0:T(8,128)(2,1)} %param.11) | copy-start | bytes 516100
  32.5 15.6 %copy-start.5 = (bf16[2,1,112,27,384]{4,2,0,3,1:T(8,128)(2,1)}, bf16[2,1,112,27,384]{4,2,0,3,1:T(8,128)(2,1)S(1)}, u32[]{:S(2)}) copy-start(bf16[2,1,112,27,384]{4,2,0,3,1:T(8,128)(2,1)S(1)} %constant_dynamic-update-slice_fusion.54) | copy-start | bytes 13934596
  32.5 16.3 %copy-start = (bf16[2,1,112,384]{3,2,1,0:T(8,128)(2,1)S(1)}, bf16[2,1,112,384]{3,2,1,0:T(8,128)(2,1)}, u32[]{:S(2)}) copy-start(bf16[2,1,112,384]{3,2,1,0:T(8,128)(2,1)} %param.10) | copy-start | bytes 516100
  32.5 16.3 %copy-start.4 = (f32[384]{0:T(512)S(1)}, f32[384]{0:T(512)}, u32[]{:S(2)}) copy-start(f32[384]{0:T(512)} %param.13) | copy-start | bytes 4612
  52.5 45.1 %copy-start.7 = (f32[384]{0:T(512)S(1)}, f32[384]{0:T(512)}, u32[]{:S(2)}) copy-start(f32[384]{0:T(512)} %param.15) | copy-start | bytes 4612
  105.0 65.0 %copy-start.6 = (f32[384]{0:T(512)S(1)}, f32[384]{0:T(512)}, u32[]{:S(2)}) copy-start(f32[384]{0:T(512)} %param.14) | copy-start | bytes 4612
  170.0 34.7 %slice-start.2 = ((s8[7962624]{0:T(1024)(128)(4,1)}), s8[4194304]{0:T(1024)(128)(4,1)S(1)}, s32[]{:S(2)}) async-start(s8[7962624]{0:T(1024)(128)(4,1)} %bitcast.529), calls=%async_computation.4 | async-start | bytes 8388608
  170.0 15.2 %copy-start.2 = (bf16[2,1,112,384]{3,2,1,0:T(8,128)(2,1)S(1)}, bf16[2,1,112,384]{3,2,1,0:T(8,128)(2,1)}, u32[]{:S(2)}) copy-start(bf16[2,1,112,384]{3,2,1,0:T(8,128)(2,1)} %param.12) | copy-start | bytes 516100
  170.0 34.6 %slice-start.3 = ((s8[7962624]{0:T(1024)(128)(4,1)}), s8[3768320]{0:T(1024)(128)(4,1)S(1)}, s32[]{:S(2)}) async-start(s8[7962624]{0:T(1024)(128)(4,1)} %bitcast.529), calls=%async_computation.5 | async-start | bytes 7536640
  178.0 13.9 %collective-permute-start.7 = (bf16[2,1,112,384]{3,2,0,1:T(8,128)(2,1)S(1)}, bf16[2,1,112,384]{3,2,0,1:T(8,128)(2,1)S(1)}, u32[]{:S(2)}, u32[]{:S(2)}) collective-permute-start(bf16[2,1,112,384]{3,2,0,1:T(8,128)(2,1)S(1)} %bitcast.541), channel_id=1, source_target_pairs={{1,0},{2,1},{3,2},{4,3},{5,4},{6,5},{7,6},{8,7},{9,8},{10,9},{11,1... | collective-permute-start | bytes 516104 | tf_op jit(solution)/shard_map/ppermute | solution.py:15
  180.2 11.7 %collective-permute-start.6 = (bf16[2,1,112,384]{3,2,0,1:T(8,128)(2,1)S(1)}, bf16[2,1,112,384]{3,2,0,1:T(8,128)(2,1)S(1)}, u32[]{:S(2)}, u32[]{:S(2)}) collective-permute-start(bf16[2,1,112,384]{3,2,0,1:T(8,128)(2,1)S(1)} %bitcast.542), channel_id=1, source_target_pairs={{0,1},{1,2},{2,3},{3,4},{4,5},{5,6},{6,7},{7,8},{8,9},{9,10},{10,1... | collective-permute-start | bytes 516104 | tf_op jit(solution)/shard_map/ppermute | solution.py:12
  185.2 25.7 %collective-permute-start.3 = (bf16[4,1,112,384]{3,2,0,1:T(8,128)(2,1)S(1)}, bf16[4,1,112,384]{3,2,0,1:T(8,128)(2,1)S(1)}, u32[]{:S(2)}, u32[]{:S(2)}) collective-permute-start(bf16[4,1,112,384]{3,2,0,1:T(8,128)(2,1)S(1)} %pad_maximum_fusion.1), channel_id=1, source_target_pairs={{1,0},{2,1},{3,2},{4,3},{5,4},{6,5},{7,6},{8,7},{9,8},{10,9},{11,1... | collective-permute-start | bytes 1032200 | tf_op jit(solution)/shard_map/ppermute | solution.py:15
  187.1 23.8 %collective-permute-start.2 = (bf16[4,1,112,384]{3,2,0,1:T(8,128)(2,1)S(1)}, bf16[4,1,112,384]{3,2,0,1:T(8,128)(2,1)S(1)}, u32[]{:S(2)}, u32[]{:S(2)}) collective-permute-start(bf16[4,1,112,384]{3,2,0,1:T(8,128)(2,1)S(1)} %pad_maximum_fusion.1), channel_id=1, source_target_pairs={{0,1},{1,2},{2,3},{3,4},{4,5},{5,6},{6,7},{7,8},{8,9},{9,10},{10,1... | collective-permute-start | bytes 1032200 | tf_op jit(solution)/shard_map/ppermute | solution.py:12
  204.6 7.8 %slice-start = ((s8[7962624]{0:T(1024)(128)(4,1)}), s8[4194304]{0:T(1024)(128)(4,1)S(1)}, s32[]{:S(2)}) async-start(s8[7962624]{0:T(1024)(128)(4,1)} %bitcast.525), calls=%async_computation.2 | async-start | bytes 8388608
  204.6 7.8 %slice-start.1 = ((s8[7962624]{0:T(1024)(128)(4,1)}), s8[3768320]{0:T(1024)(128)(4,1)S(1)}, s32[]{:S(2)}) async-start(s8[7962624]{0:T(1024)(128)(4,1)} %bitcast.525), calls=%async_computation.3 | async-start | bytes 7536640
  211.2 1.2 copy-start.8
Sparse Core Ops, SparseCore 0:
  10.2 76.0 all-gather.2
  88.4 70.2 all-gather.4
where the time goes:
time: 223 us
  waiting for transfers between devices  89.8 us (40%)
  local copies, waits for them, and re-layouts  61.4 us (28%)
  starting transfers between devices  26.1 us (12%)
  matrix products  23.8 us (11%)
  between operations  14.6 us (7%)
  other arithmetic  6.78 us (3%)
    all_gather x1, waiting for transfers between devices, local(): lax.all_gather(weight_second, 'ha', axis=1, tiled=True)  53.7 us
    unnamed x127, local copies, waits for them, and re-layouts  37.3 us
    all_gather x1, waiting for transfers between devices, local(): lax.all_gather(weight_first, 'ha', axis=1, tiled=True)  33.8 us
    ppermute x4, starting transfers between devices, extended_2(): lax.ppermute(lax.slice_in_dim(block, block.shape[dim] - width, None, axis...  17.4 us
    all_gather x1, local copies, waits for them, and re-layouts, local(): lax.all_gather(weight_first, 'ha', axis=1, tiled=True)  11.3 us
    all_gather x1, local copies, waits for them, and re-layouts, local(): lax.all_gather(weight_second, 'ha', axis=1, tiled=True)  11.3 us
    ppermute x4, starting transfers between devices, extended_2(): lax.ppermute(lax.slice_in_dim(block, 0, width, axis=dim), axis, backward)  8.6 us
    dot_general x1, matrix products, local(): jnp.einsum('lrwto,tco->lrwc', patches, kernel_two, preferred_element_type...  7.75 us
  transfers between devices with their start and end apart: 10, of which 4 were waited for; matrix products, arithmetic and copies ran while one was open for 31% of the time, Pallas kernels for 0%

commit v1 on v0

--- a/solution.py
+++ b/solution.py
@@ -68,7 +68,9 @@
 ):
     length, rows, columns, channels = frames.shape
     kernel_one, kernel_two = (
-        lax.all_gather(weight_first, "ha", axis=1, tiled=True),
+        jnp.concatenate(
+            lax.all_to_all(jnp.stack([weight_first] * lax.axis_size("ha")), "ha", 0, 0), axis=1
+        ),
         lax.all_gather(weight_second, "ha", axis=1, tiled=True),
     )
     kernel_one = kernel_one.reshape(27, channels, channels)

time: 223 us -> 369 us (1.65)
  the two profiles are of different devices: /device:TPU:5 before, /device:TPU:16 now
where the time goes in v1:
time: 369 us; the launch traced here: 368 us
  waiting for transfers between devices  208 us (56%)
  local copies, waits for them, and re-layouts  81.6 us (22%)
  starting transfers between devices  32.7 us (9%)
  matrix products  26.9 us (7%)
  between operations  14.7 us (4%)
  other arithmetic  4.06 us (1%)
    ppermute x4, waiting for transfers between devices, extended_2(): lax.ppermute(lax.slice_in_dim(block, block.shape[dim] - width, None, axis...  207 us
    unnamed x129, local copies, waits for them, and re-layouts  37.2 us
    another operation x2, local copies, waits for them, and re-layouts, local(): kernel_one = kernel_one.reshape(27, channels, channels)  26.9 us
    ppermute x4, starting transfers between devices, extended_2(): lax.ppermute(lax.slice_in_dim(block, 0, width, axis=dim), axis, backward)  18.2 us
    all_gather x1, local copies, waits for them, and re-layouts, local(): lax.all_gather(weight_second, 'ha', axis=1, tiled=True)  11.3 us
    dot_general x1, matrix products, local(): jnp.einsum('lrwto,tco->lrwc', patches, kernel_one, preferred_element_type...  8.51 us
    ppermute x4, starting transfers between devices, extended_2(): lax.ppermute(lax.slice_in_dim(block, block.shape[dim] - width, None, axis...  8.05 us
    dot_general x1, matrix products, local(): jnp.einsum('lrwto,tco->lrwc', patches, kernel_two, preferred_element_type...  7.72 us
  transfers between devices with their start and end apart: 10, of which 1 were waited for; matrix products, arithmetic and copies ran while one was open for 23% of the time, Pallas kernels for 0%

profile of v1, /device:TPU:16, one launch (start us, length us, event | category | flops | bytes accessed | tf_op | source)
XLA Modules:
  0.0 367.5 jit_solution(12871437953055186392)
XLA Ops:
  7.2 4.6 %stack.349 = bf16[16,10368,24]{1,2,0:T(8,128)(2,1)} broadcast(bf16[10368,24]{0,1:T(8,128)(2,1)} %param.17), dimensions={1,2} | broadcast | bytes 8460288 | tf_op jit(solution)/shard_map/stack | solution.py:72
  11.8 6.3 %all-to-all-start = ((bf16[16,10368,24]{1,2,0:T(8,128)(2,1)}), bf16[16,10368,24]{1,2,0:T(8,128)(2,1)}, u32[]{:S(2)}, u32[]{:S(2)}) async-start(bf16[16,10368,24]{1,2,0:T(8,128)(2,1)} %stack.349), calls=%async_computation | async-start | bytes 15925248 | tf_op jit(solution)/shard_map/all_to_all | solution.py:72
  19.3 2.0 collective-permute-start
  21.3 4.4 %collective-permute-start.1 = (bf16[4,1,112,384]{3,2,0,1:T(8,128)(2,1)S(1)}, bf16[4,1,112,384]{3,2,0,1:T(8,128)(2,1)S(1)}, u32[]{:S(2)}, u32[]{:S(2)}) collective-permute-start(bf16[4,1,112,384]{3,2,0,1:T(8,128)(2,1)S(1)} %pad_maximum_fusion), channel_id=1, source_target_pairs={{1,0},{2,1},{3,2},{4,3},{5,4},{6,5},{7,6},{8,7},{9,8},{10,9},{11,1... | collective-permute-start | bytes 1032200 | tf_op jit(solution)/shard_map/ppermute | solution.py:15
  25.8 1.9 collective-permute-start.4
  27.7 4.5 %collective-permute-start.5 = (bf16[2,1,112,384]{3,2,0,1:T(8,128)(2,1)S(1)}, bf16[2,1,112,384]{3,2,0,1:T(8,128)(2,1)S(1)}, u32[]{:S(2)}, u32[]{:S(2)}) collective-permute-start(bf16[2,1,112,384]{3,2,0,1:T(8,128)(2,1)S(1)} %bitcast.554), channel_id=1, source_target_pairs={{1,0},{2,1},{3,2},{4,3},{5,4},{6,5},{7,6},{8,7},{9,8},{10,9},{11,1... | collective-permute-start | bytes 516104 | tf_op jit(solution)/shard_map/ppermute | solution.py:15
  38.0 207.0 %collective-permute-done.4 = bf16[2,1,112,384]{3,2,0,1:T(8,128)(2,1)S(1)} collective-permute-done((bf16[2,1,112,384]{3,2,0,1:T(8,128)(2,1)S(1)}, bf16[2,1,112,384]{3,2,0,1:T(8,128)(2,1)S(1)}, u32[]{:S(2)}, u32[]{:S(2)}) %collective-permute-start.4) | collective-permute-done | bytes 172064 | tf_op jit(solution)/shard_map/ppermute | solution.py:12
  246.4 1.0 constant_dynamic-update-slice_fusion.26
  247.4 0.9 constant_dynamic-update-slice_fusion.25
  248.3 0.7 constant_dynamic-update-slice_fusion.24
  249.7 0.7 constant_dynamic-update-slice_fusion.22
  250.4 0.7 constant_dynamic-update-slice_fusion.21
  251.1 0.7 constant_dynamic-update-slice_fusion.20
  252.5 0.7 constant_dynamic-update-slice_fusion.18
  253.9 0.7 constant_dynamic-update-slice_fusion.16
  254.6 0.7 constant_dynamic-update-slice_fusion.15
  256.0 0.7 constant_dynamic-update-slice_fusion.13
  256.7 0.7 constant_dynamic-update-slice_fusion.12
  257.4 0.7 constant_dynamic-update-slice_fusion.11
  258.8 0.7 constant_dynamic-update-slice_fusion.9
  259.5 0.7 constant_dynamic-update-slice_fusion.8
  260.2 0.7 constant_dynamic-update-slice_fusion.7
  260.9 0.7 constant_dynamic-update-slice_fusion.6
  262.3 0.9 constant_dynamic-update-slice_fusion.4
  263.2 0.7 constant_dynamic-update-slice_fusion.3
  265.2 0.7 constant_dynamic-update-slice_fusion
  266.0 13.8 %reshape_reshape.3 = bf16[27,384,384]{1,0,2:T(8,128)(2,1)} reshape(bf16[10368,16,24]{0,2,1:T(8,128)(2,1)} %bitcast.56) | data formatting | bytes 15925248 | tf_op jit(solution)/shard_map/reshape;reshape | solution.py:76
  279.7 13.1 %copy.78 = bf16[27,384,384]{2,1,0:T(8,128)(2,1)} copy(bf16[27,384,384]{1,0,2:T(8,128)(2,1)} %reshape_reshape.3) | data formatting | bytes 15925248 | tf_op jit(solution)/shard_map/reshape;reshape | solution.py:76
  292.8 7.4 %multiply_reduce_fusion.1 = (f32[2,112]{1,0:T(2,128)S(1)}, f32[2,112,384]{2,1,0:T(8,128)S(1)}) fusion(f32[384]{0:T(512)S(1)} %copy-done.7, bf16[27,384,384]{2,1,0:T(8,128)(2,1)} %copy.78, bf16[2,1,112,27,384]{4,2,3,0,1:T(8,128)(2,1)} %constant_dynamic-update-slice_fusion), kind=kOutput, calls=%fused_computation.92 | convolution fusion | flops 1784057600 | bytes 12953984 | tf_op jit(solution)/shard_map/lrwtc,tco->lrwo/dot_general | solution.py:83
  300.3 11.3 %copy.80 = bf16[10368,384]{1,0:T(8,128)(2,1)} copy(bf16[10368,384]{0,1:T(8,128)(2,1)} %all-gather.2.cloned.1.call-done) | data formatting | bytes 15925248 | tf_op jit(solution)/shard_map/all_gather | solution.py:74
  311.6 7.7 %multiply_reduce_fusion = (f32[2,112]{1,0:T(2,128)S(1)}, f32[2,112,384]{2,1,0:T(8,128)S(1)}) fusion(f32[2,112,384]{2,1,0:T(8,128)S(1)} %get-tuple-element.13, f32[2,112]{1,0:T(2,128)S(1)} %get-tuple-element.11, bf16[27,384,384,1]{2,1,3,0:T(8,128)(2,1)} %bitcast.537, bf16[2,1,112,27,384]{4,2,0,3,1:T(8,128)(2,1)} %copy-done.5, f32[384]{0:T(512)S(1)} %copy-done.6), kind=kOutput, calls=%fused_computation.88 | convolution fusion | flops 1784745728 | bytes 13298944 | tf_op jit(solution)/shard_map/lrwto,tco->lrwc/dot_general | solution.py:99
  319.6 2.2 collective-permute-start.6
  321.8 4.5 %collective-permute-start.7 = (bf16[2,1,112,384]{3,2,0,1:T(8,128)(2,1)S(1)}, bf16[2,1,112,384]{3,2,0,1:T(8,128)(2,1)S(1)}, u32[]{:S(2)}, u32[]{:S(2)}) collective-permute-start(bf16[2,1,112,384]{3,2,0,1:T(8,128)(2,1)S(1)} %bitcast.551), channel_id=1, source_target_pairs={{1,0},{2,1},{3,2},{4,3},{5,4},{6,5},{7,6},{8,7},{9,8},{10,9},{11,1... | collective-permute-start | bytes 516104 | tf_op jit(solution)/shard_map/ppermute | solution.py:15
  327.0 1.9 collective-permute-start.2
  329.0 4.7 %collective-permute-start.3 = (bf16[4,1,112,384]{3,2,0,1:T(8,128)(2,1)S(1)}, bf16[4,1,112,384]{3,2,0,1:T(8,128)(2,1)S(1)}, u32[]{:S(2)}, u32[]{:S(2)}) collective-permute-start(bf16[4,1,112,384]{3,2,0,1:T(8,128)(2,1)S(1)} %pad_maximum_fusion.1), channel_id=1, source_target_pairs={{1,0},{2,1},{3,2},{4,3},{5,4},{6,5},{7,6},{8,7},{9,8},{10,9},{11,1... | collective-permute-start | bytes 1032200 | tf_op jit(solution)/shard_map/ppermute | solution.py:15
  333.9 0.7 constant_dynamic-update-slice_fusion.98
  334.6 0.7 constant_dynamic-update-slice_fusion.97
  336.0 0.7 constant_dynamic-update-slice_fusion.95
  336.7 0.7 constant_dynamic-update-slice_fusion.94
  338.1 0.7 constant_dynamic-update-slice_fusion.92
  338.8 0.7 constant_dynamic-update-slice_fusion.91
  340.2 0.7 constant_dynamic-update-slice_fusion.89
  341.6 0.7 constant_dynamic-update-slice_fusion.87
  342.3 0.7 constant_dynamic-update-slice_fusion.86
  344.4 0.7 constant_dynamic-update-slice_fusion.83
  346.5 8.5 %fusion.125 = (f32[2,112]{1,0:T(2,128)S(1)}, f32[2,1,112,384]{3,2,0,1:T(8,128)S(1)}) fusion(bf16[2,1,112,384]{3,2,1,0:T(8,128)(2,1)S(1)} %copy-done, f32[384]{0:T(512)S(1)} %copy-done.4, f32[2,112]{1,0:T(2,128)S(1)} %get-tuple-element.9, bf16[27,384,384,1]{1,0,2,3:T(8,128)(2,1)S(1)} %bitcast.536, ...), kind=kOutput, calls=%fused_computation.86 | convolution fusion | flops 1784831744 | bytes 13126912 | tf_op jit(solution)/shard_map/lrwto,tco->lrwc/dot_general | solution.py:106
  355.0 0.8 fusion.126
  357.4 3.3 fusion.88
  (133 shorter events, 21.5 us)
Async XLA Ops:
  11.8 7.1 %copy-start = (bf16[2,1,112,384]{3,2,1,0:T(8,128)(2,1)S(1)}, bf16[2,1,112,384]{3,2,1,0:T(8,128)(2,1)}, u32[]{:S(2)}) copy-start(bf16[2,1,112,384]{3,2,1,0:T(8,128)(2,1)} %param.10) | copy-start | bytes 516100
  11.8 7.2 %copy-start.4 = (f32[384]{0:T(512)S(1)}, f32[384]{0:T(512)}, u32[]{:S(2)}) copy-start(f32[384]{0:T(512)} %param.13) | copy-start | bytes 4612
  11.8 7.4 %copy-start.1 = (bf16[2,1,112,384]{3,2,1,0:T(8,128)(2,1)S(1)}, bf16[2,1,112,384]{3,2,1,0:T(8,128)(2,1)}, u32[]{:S(2)}) copy-start(bf16[2,1,112,384]{3,2,1,0:T(8,128)(2,1)} %param.11) | copy-start | bytes 516100
  11.8 13.9 %copy-start.3 = (bf16[2,1,112,384]{3,2,1,0:T(8,128)(2,1)S(1)}, bf16[2,1,112,384]{3,2,1,0:T(8,128)(2,1)}, u32[]{:S(2)}) copy-start(bf16[2,1,112,384]{3,2,1,0:T(8,128)(2,1)} %param.19) | copy-start | bytes 516100
  11.8 254.1 %all-to-all-start = ((bf16[16,10368,24]{1,2,0:T(8,128)(2,1)}), bf16[16,10368,24]{1,2,0:T(8,128)(2,1)}, u32[]{:S(2)}, u32[]{:S(2)}) async-start(bf16[16,10368,24]{1,2,0:T(8,128)(2,1)} %stack.349), calls=%async_computation | async-start | bytes 15925248 | tf_op jit(solution)/shard_map/all_to_all | solution.py:72
  18.1 282.1 %all-gather.2.cloned.1.call-start = ((), (), s32[]{:S(2)}) async-start(), calls=%async_computation.1 | async-start | bytes 8460288 | tf_op jit(solution)/shard_map/all_gather | solution.py:74
  19.3 226.8 %collective-permute-start = (bf16[4,1,112,384]{3,2,0,1:T(8,128)(2,1)S(1)}, bf16[4,1,112,384]{3,2,0,1:T(8,128)(2,1)S(1)}, u32[]{:S(2)}, u32[]{:S(2)}) collective-permute-start(bf16[4,1,112,384]{3,2,0,1:T(8,128)(2,1)S(1)} %pad_maximum_fusion), channel_id=1, source_target_pairs={{0,1},{1,2},{2,3},{3,4},{4,5},{5,6},{6,7},{7,8},{8,9},{9,10},{10,1... | collective-permute-start | bytes 1032200 | tf_op jit(solution)/shard_map/ppermute | solution.py:12
  21.3 224.8 %collective-permute-start.1 = (bf16[4,1,112,384]{3,2,0,1:T(8,128)(2,1)S(1)}, bf16[4,1,112,384]{3,2,0,1:T(8,128)(2,1)S(1)}, u32[]{:S(2)}, u32[]{:S(2)}) collective-permute-start(bf16[4,1,112,384]{3,2,0,1:T(8,128)(2,1)S(1)} %pad_maximum_fusion), channel_id=1, source_target_pairs={{1,0},{2,1},{3,2},{4,3},{5,4},{6,5},{7,6},{8,7},{9,8},{10,9},{11,1... | collective-permute-start | bytes 1032200 | tf_op jit(solution)/shard_map/ppermute | solution.py:15
  25.8 219.2 %collective-permute-start.4 = (bf16[2,1,112,384]{3,2,0,1:T(8,128)(2,1)S(1)}, bf16[2,1,112,384]{3,2,0,1:T(8,128)(2,1)S(1)}, u32[]{:S(2)}, u32[]{:S(2)}) collective-permute-start(bf16[2,1,112,384]{3,2,0,1:T(8,128)(2,1)S(1)} %bitcast.553), channel_id=1, source_target_pairs={{0,1},{1,2},{2,3},{3,4},{4,5},{5,6},{6,7},{7,8},{8,9},{9,10},{10,1... | collective-permute-start | bytes 516104 | tf_op jit(solution)/shard_map/ppermute | solution.py:12
  27.7 217.3 %collective-permute-start.5 = (bf16[2,1,112,384]{3,2,0,1:T(8,128)(2,1)S(1)}, bf16[2,1,112,384]{3,2,0,1:T(8,128)(2,1)S(1)}, u32[]{:S(2)}, u32[]{:S(2)}) collective-permute-start(bf16[2,1,112,384]{3,2,0,1:T(8,128)(2,1)S(1)} %bitcast.554), channel_id=1, source_target_pairs={{1,0},{2,1},{3,2},{4,3},{5,4},{6,5},{7,6},{8,7},{9,8},{10,9},{11,1... | collective-permute-start | bytes 516104 | tf_op jit(solution)/shard_map/ppermute | solution.py:15
  246.0 15.6 %copy-start.5 = (bf16[2,1,112,27,384]{4,2,0,3,1:T(8,128)(2,1)}, bf16[2,1,112,27,384]{4,2,0,3,1:T(8,128)(2,1)S(1)}, u32[]{:S(2)}) copy-start(bf16[2,1,112,27,384]{4,2,0,3,1:T(8,128)(2,1)S(1)} %constant_dynamic-update-slice_fusion.54) | copy-start | bytes 13934596
  279.7 13.1 %copy-start.7 = (f32[384]{0:T(512)S(1)}, f32[384]{0:T(512)}, u32[]{:S(2)}) copy-start(f32[384]{0:T(512)} %param.15) | copy-start | bytes 4612
  300.2 11.4 %copy-start.6 = (f32[384]{0:T(512)S(1)}, f32[384]{0:T(512)}, u32[]{:S(2)}) copy-start(f32[384]{0:T(512)} %param.14) | copy-start | bytes 4612
  311.6 15.4 %copy-start.2 = (bf16[2,1,112,384]{3,2,1,0:T(8,128)(2,1)S(1)}, bf16[2,1,112,384]{3,2,1,0:T(8,128)(2,1)}, u32[]{:S(2)}) copy-start(bf16[2,1,112,384]{3,2,1,0:T(8,128)(2,1)} %param.12) | copy-start | bytes 516100
  311.6 34.8 %slice-start = ((s8[9437184]{0:T(1024)(128)(4,1)}), s8[4194304]{0:T(1024)(128)(4,1)S(1)}, s32[]{:S(2)}) async-start(s8[9437184]{0:T(1024)(128)(4,1)} %bitcast.534), calls=%async_computation.2 | async-start | bytes 8388608
  311.6 34.8 %slice-start.1 = ((s8[9437184]{0:T(1024)(128)(4,1)}), s8[1048576]{0:T(1024)(128)(4,1)S(1)}, s32[]{:S(2)}) async-start(s8[9437184]{0:T(1024)(128)(4,1)} %bitcast.534), calls=%async_computation.3 | async-start | bytes 2097152
  319.6 26.9 %slice-start.2 = ((s8[9437184]{0:T(1024)(128)(4,1)}), s8[4194304]{0:T(1024)(128)(4,1)S(1)}, s32[]{:S(2)}) async-start(s8[9437184]{0:T(1024)(128)(4,1)} %bitcast.534), calls=%async_computation.4 | async-start | bytes 8388608
  319.6 14.1 %collective-permute-start.6 = (bf16[2,1,112,384]{3,2,0,1:T(8,128)(2,1)S(1)}, bf16[2,1,112,384]{3,2,0,1:T(8,128)(2,1)S(1)}, u32[]{:S(2)}, u32[]{:S(2)}) collective-permute-start(bf16[2,1,112,384]{3,2,0,1:T(8,128)(2,1)S(1)} %bitcast.550), channel_id=1, source_target_pairs={{0,1},{1,2},{2,3},{3,4},{4,5},{5,6},{6,7},{7,8},{8,9},{9,10},{10,1... | collective-permute-start | bytes 516104 | tf_op jit(solution)/shard_map/ppermute | solution.py:12
  321.8 11.9 %collective-permute-start.7 = (bf16[2,1,112,384]{3,2,0,1:T(8,128)(2,1)S(1)}, bf16[2,1,112,384]{3,2,0,1:T(8,128)(2,1)S(1)}, u32[]{:S(2)}, u32[]{:S(2)}) collective-permute-start(bf16[2,1,112,384]{3,2,0,1:T(8,128)(2,1)S(1)} %bitcast.551), channel_id=1, source_target_pairs={{1,0},{2,1},{3,2},{4,3},{5,4},{6,5},{7,6},{8,7},{9,8},{10,9},{11,1... | collective-permute-start | bytes 516104 | tf_op jit(solution)/shard_map/ppermute | solution.py:15
  327.0 28.8 %collective-permute-start.2 = (bf16[4,1,112,384]{3,2,0,1:T(8,128)(2,1)S(1)}, bf16[4,1,112,384]{3,2,0,1:T(8,128)(2,1)S(1)}, u32[]{:S(2)}, u32[]{:S(2)}) collective-permute-start(bf16[4,1,112,384]{3,2,0,1:T(8,128)(2,1)S(1)} %pad_maximum_fusion.1), channel_id=1, source_target_pairs={{0,1},{1,2},{2,3},{3,4},{4,5},{5,6},{6,7},{7,8},{8,9},{9,10},{10,1... | collective-permute-start | bytes 1032200 | tf_op jit(solution)/shard_map/ppermute | solution.py:12
  329.0 26.9 %collective-permute-start.3 = (bf16[4,1,112,384]{3,2,0,1:T(8,128)(2,1)S(1)}, bf16[4,1,112,384]{3,2,0,1:T(8,128)(2,1)S(1)}, u32[]{:S(2)}, u32[]{:S(2)}) collective-permute-start(bf16[4,1,112,384]{3,2,0,1:T(8,128)(2,1)S(1)} %pad_maximum_fusion.1), channel_id=1, source_target_pairs={{1,0},{2,1},{3,2},{4,3},{5,4},{6,5},{7,6},{8,7},{9,8},{10,9},{11,1... | collective-permute-start | bytes 1032200 | tf_op jit(solution)/shard_map/ppermute | solution.py:15
  346.4 10.9 %slice-start.3 = ((s8[7962624]{0:T(1024)(128)(4,1)}), s8[4194304]{0:T(1024)(128)(4,1)S(1)}, s32[]{:S(2)}) async-start(s8[7962624]{0:T(1024)(128)(4,1)} %bitcast.538), calls=%async_computation.5 | async-start | bytes 8388608
  346.5 10.9 %slice-start.4 = ((s8[7962624]{0:T(1024)(128)(4,1)}), s8[3768320]{0:T(1024)(128)(4,1)S(1)}, s32[]{:S(2)}) async-start(s8[7962624]{0:T(1024)(128)(4,1)} %bitcast.538), calls=%async_computation.6 | async-start | bytes 7536640
  356.2 1.2 copy-start.8
Sparse Core Ops, SparseCore 0:
  21.1 171.0 all-gather.1
